TPU v7x, 64 devices: a 2x2x8 block of a 4x4x8 slice. The times are simulated.
64 devices in a mesh: rep: 8 (over x, y, core), dp: 8 (over z).
Axes of the slice: x: 2, y: 2, z: 8, core: 2. Of those that a mesh axis runs over, the one named last changes fastest.
The devices are a block of a 4x4x8 slice.
Arguments:
- x: bfloat16 [64, 2048, 512], P(('rep', 'dp')), parts along dimension 0
- dy: bfloat16 [64, 2048, 512], P(('rep', 'dp')), parts along dimension 0
- w_gate: bfloat16 [2, 512, 2048], P(None, 'dp')
- w_up: bfloat16 [2, 512, 2048], P(None, 'dp')
- w_down: bfloat16 [2, 2048, 512], P(None, 'dp')
Outputs:
- output 1: bfloat16 [64, 2048, 512], P(('rep', 'dp')), parts along dimension 0
- output 2: bfloat16 [16, 512, 2048], P('rep', 'dp'), parts along dimension 0
- output 3: bfloat16 [16, 512, 2048], P('rep', 'dp'), parts along dimension 0
- output 4: bfloat16 [16, 2048, 512], P('rep', 'dp'), parts along dimension 0
There are 8 independent parts. A program takes and returns all parts, laid end to end along the dimension named above; an argument that names none is the same for every part.
All inputs are finite; a program needn't handle non-finite values.
Results may differ from a plain program's by a relative error of at most 0.018.
Values are sent between devices in bfloat16 or wider.
A program may use at most 768 MiB of HBM per device.

v0:
```python
import jax
import jax.numpy as jnp
from jax import lax

NAMES = ("w_gate", "w_up", "w_down")


def matmul(a, w):
    return jnp.dot(a, w, preferred_element_type=jnp.float32).astype(jnp.bfloat16)


def normed(h):
    wide = h.astype(jnp.float32)
    scale = lax.rsqrt(jnp.mean(wide**2, -1, keepdims=True) + 1e-6)
    return (wide * scale).astype(jnp.bfloat16)


def layer(h, w):
    a = normed(h)
    gate = jnp.dot(a, w["w_gate"], preferred_element_type=jnp.float32)
    up = jnp.dot(a, w["w_up"], preferred_element_type=jnp.float32)
    return h + matmul((jax.nn.silu(gate) * up).astype(jnp.bfloat16), w["w_down"])


def stack(weights, h):
    for number in range(weights["w_gate"].shape[0]):
        h = layer(h, {name: w[number] for name, w in weights.items()})
    return h


def solution(mesh):
    groups = mesh.shape["rep"]

    def step(x, dy, *weights):
        shape = x.shape
        x, dy = (t.reshape(groups, -1, *t.shape[1:]) for t in (x, dy))

        def of_a_group(x, dy):
            _, back = jax.vjp(stack, dict(zip(NAMES, weights, strict=True)), x)
            by_weights, by_x = back(dy)
            return (by_x, *(by_weights[name] for name in NAMES))

        by_x, *by_weights = jax.vmap(of_a_group)(x, dy)
        return (by_x.reshape(shape), *(t.reshape(-1, *t.shape[2:]) for t in by_weights))

    return step
```

profile of v0, /device:TPU:28, one launch (start us, length us, event | category | flops | bytes accessed | tf_op | source)
XLA Modules:
  0.0 620.7 jit_solution(570160160839934173)
XLA Ops:
  7.3 2.0 fusion.104
  9.4 1.9 fusion.103
  11.4 1.9 fusion.105
  15.8 2.4 copy.1
  18.8 3.9 copy
  22.7 28.1 %all-gather.29.cloned.1.call-done = bf16[1,512,2048]{2,1,0:T(8,128)(2,1)} async-done(((bf16[1,64,2048]{2,1,0:T(8,128)(2,1)}), bf16[1,512,2048]{2,1,0:T(8,128)(2,1)}) %all-gather.29.cloned.1.call-update) | async-done | bytes 2097168 | tf_op jit(solution)/vmap(jvp())/squeeze | solution.py:27
  50.8 9.7 %fusion.87 = f32[2048,2048]{1,0:T(8,128)} fusion(bf16[1,512,2048]{2,1,0:T(8,128)(2,1)} %all-gather.29.cloned.1.call-done, bf16[1,2048,512]{2,1,0:T(8,128)(2,1)S(1)} %copy-done.2, f32[2048]{0:T(1024)S(1)} %get-tuple-element.13), kind=kOutput, calls=%fused_computation.105 | convolution fusion | flops 4298113024 | bytes 20979712 | tf_op jit(solution)/vmap(jvp())/dot_general | solution.py:20
  60.5 28.3 %all-gather.31.cloned.1.call-done = bf16[1,512,2048]{2,1,0:T(8,128)(2,1)} async-done(((bf16[1,64,2048]{2,1,0:T(8,128)(2,1)}), bf16[1,512,2048]{2,1,0:T(8,128)(2,1)}) %all-gather.31.cloned.1.call-update) | async-done | bytes 2097168 | tf_op jit(solution)/vmap(jvp())/squeeze | solution.py:27
  88.8 11.0 %fusion.84 = f32[2048,2048]{1,0:T(8,128)} fusion(bf16[1,512,2048]{2,1,0:T(8,128)(2,1)} %all-gather.31.cloned.1.call-done, bf16[1,2048,512]{2,1,0:T(8,128)(2,1)S(1)} %copy-done.2, f32[2048]{0:T(1024)S(1)} %get-tuple-element.13), kind=kOutput, calls=%fused_computation.102 | convolution fusion | flops 4298113024 | bytes 20979712 | tf_op jit(solution)/vmap(jvp())/dot_general | solution.py:21
  99.8 11.3 %fusion.24 = bf16[2048,2048]{1,0:T(8,128)(2,1)} fusion(f32[2048,2048]{1,0:T(8,128)} %fusion.84, f32[2048,2048]{1,0:T(8,128)S(1)} %copy-done), kind=kLoop, calls=%fused_computation.34 | loop fusion | flops 25165824 | bytes 41943040
  111.1 15.1 %all-gather.33.cloned.1.call-done = bf16[1,2048,512]{2,1,0:T(8,128)(2,1)} async-done(((bf16[1,256,512]{2,1,0:T(8,128)(2,1)}), bf16[1,2048,512]{2,1,0:T(8,128)(2,1)}) %all-gather.33.cloned.1.call-update) | async-done | bytes 2097168 | tf_op jit(solution)/vmap(jvp())/squeeze | solution.py:27
  126.3 10.2 %fusion.40 = (f32[2048]{0:T(1024)S(1)}, bf16[1,1,2048,512]{2,3,1,0:T(8,128)(2,1)}) fusion(bf16[2048,2048]{1,0:T(8,128)(2,1)} %fusion.24, bf16[1,2048,512]{2,1,0:T(8,128)(2,1)} %all-gather.33.cloned.1.call-done, bf16[1,2048,512]{1,2,0:T(8,128)(2,1)S(1)} %copy-done.3), kind=kOutput, calls=%fused_computation.62 | convolution fusion | flops 4300208128 | bytes 14688256 | tf_op jit(solution)/vmap(jvp())/dot_general | solution.py:9
  136.5 27.0 %all-gather.37.cloned.1.call-done = bf16[1,2048,512]{2,1,0:T(8,128)(2,1)} async-done(((bf16[1,256,512]{2,1,0:T(8,128)(2,1)}), bf16[1,2048,512]{2,1,0:T(8,128)(2,1)}) %all-gather.37.cloned.1.call-update) | async-done | bytes 2097168 | tf_op jit(solution)/vmap(jvp())/squeeze | solution.py:27
  163.5 10.0 %convolution_convert_fusion.1 = bf16[2048,2048]{1,0:T(8,128)(2,1)} fusion(bf16[1,2048,512]{2,1,0:T(8,128)(2,1)} %all-gather.37.cloned.1.call-done, bf16[1,2048,512]{2,1,0:T(8,128)(2,1)} %param), kind=kOutput, calls=%fused_computation.42 | convolution fusion | flops 4299161600 | bytes 12582912 | tf_op jit(solution)/vmap(transpose(jvp()))/dot_general | solution.py:9
  173.6 27.8 %all-gather.35.cloned.1.call-done = bf16[1,512,2048]{2,1,0:T(8,128)(2,1)} async-done(((bf16[1,64,2048]{2,1,0:T(8,128)(2,1)}), bf16[1,512,2048]{2,1,0:T(8,128)(2,1)}) %all-gather.35.cloned.1.call-update) | async-done | bytes 2097168 | tf_op jit(solution)/vmap(jvp())/squeeze | solution.py:27
  201.4 9.7 %fusion.79 = f32[2048,2048]{1,0:T(8,128)} fusion(bf16[1,512,2048]{2,1,0:T(8,128)(2,1)} %all-gather.35.cloned.1.call-done, bf16[1,1,2048,512]{2,3,1,0:T(8,128)(2,1)S(1)} %copy-done.9, f32[2048]{0:T(1024)S(1)} %bitcast.266), kind=kOutput, calls=%fused_computation.97 | convolution fusion | flops 4298113024 | bytes 20979712 | tf_op jit(solution)/vmap(jvp())/dot_general | solution.py:20
  211.1 28.1 %all-gather.39.cloned.1.call-done = bf16[1,512,2048]{2,1,0:T(8,128)(2,1)} async-done(((bf16[1,64,2048]{2,1,0:T(8,128)(2,1)}), bf16[1,512,2048]{2,1,0:T(8,128)(2,1)}) %all-gather.39.cloned.1.call-update) | async-done | bytes 2097168 | tf_op jit(solution)/vmap(jvp())/squeeze | solution.py:27
  239.3 10.9 %fusion.72 = f32[2048,2048]{1,0:T(8,128)} fusion(bf16[1,512,2048]{2,1,0:T(8,128)(2,1)} %all-gather.39.cloned.1.call-done, bf16[1,1,2048,512]{2,3,1,0:T(8,128)(2,1)S(1)} %copy-done.9, f32[2048]{0:T(1024)S(1)} %bitcast.267), kind=kOutput, calls=%fused_computation.90 | convolution fusion | flops 4298113024 | bytes 20979712 | tf_op jit(solution)/vmap(jvp())/dot_general | solution.py:21
  250.2 14.0 %fusion.4 = bf16[2048,2048]{1,0:T(8,128)(2,1)} fusion(f32[2048,2048]{1,0:T(8,128)S(1)} %copy-done.1, f32[2048,2048]{1,0:T(8,128)} %fusion.72, bf16[2048,2048]{1,0:T(8,128)(2,1)} %convolution_convert_fusion.1), kind=kLoop, calls=%fused_computation.10 | loop fusion | flops 50331648 | bytes 50331648
  264.2 10.2 %fusion.52 = bf16[2048,512]{0,1:T(8,128)(2,1)} fusion(bf16[2048,2048]{1,0:T(8,128)(2,1)} %convolution_convert_fusion.1, f32[2048,2048]{1,0:T(8,128)S(1)} %copy-done.1, bf16[1,512,2048]{2,1,0:T(8,128)(2,1)} %all-gather.39.cloned.1.call-done), kind=kOutput, calls=%fused_computation.72 | convolution fusion | flops 4321181696 | bytes 29360128 | tf_op jit(solution)/vmap(transpose(jvp()))/dot_general | solution.py:21
  274.4 9.6 %fusion.42 = (f32[2048]{0:T(1024)S(1)}, bf16[1,1,2048,512]{2,3,1,0:T(8,128)(2,1)S(1)}) fusion(bf16[1,1,2048,512]{2,3,1,0:T(8,128)(2,1)S(1)} %copy-done.9, bf16[2048,512]{0,1:T(8,128)(2,1)} %fusion.52, bf16[2048,2048]{1,0:T(8,128)(2,1)} %fusion.4, bf16[1,512,2048]{2,1,0:T(8,128)(2,1)} %all-gather.35.cloned.1.call-done), kind=kOutput, calls=%fused_computation.64 | convolution fusion | flops 4300208128 | bytes 16785408 | tf_op jit(solution)/vmap(transpose(jvp()))/dot_general | solution.py:20
  284.1 1.4 fusion.68
  285.5 10.5 %convolution_bitcast_fusion.2 = f32[1,2048,512]{2,1,0:T(8,128)} fusion(bf16[2048,2048]{1,0:T(8,128)(2,1)} %fusion.24, bf16[1,1,2048,512]{2,3,1,0:T(8,128)(2,1)S(1)} %fusion.68), kind=kOutput, calls=%fused_computation.68 | convolution fusion | flops 4294967296 | bytes 14680064 | tf_op jit(solution)/vmap(transpose(jvp()))/dot_general | solution.py:9
  296.1 15.7 %fusion.43 = f32[1,2048,512]{2,1,0:T(8,128)} fusion(f32[2048,2048]{1,0:T(8,128)} %fusion.72, f32[2048,2048]{1,0:T(8,128)} %fusion.79, bf16[1,2048,512]{2,1,0:T(8,128)(2,1)} %param), kind=kOutput, calls=%fused_computation.65 | convolution fusion | flops 4320133120 | bytes 39845888 | tf_op jit(solution)/vmap(transpose(jvp()))/dot_general | solution.py:9
  312.1 10.5 %convolution_bitcast_fusion.1 = f32[1,512,2048]{2,1,0:T(8,128)} fusion(bf16[2048,2048]{1,0:T(8,128)(2,1)} %fusion.4, bf16[1,1,2048,512]{2,3,1,0:T(8,128)(2,1)} %get-tuple-element.15, f32[2048]{0:T(1024)S(1)} %bitcast.269), kind=kOutput, calls=%fused_computation.67 | convolution fusion | flops 4298113024 | bytes 14688256 | tf_op jit(solution)/vmap(transpose(jvp()))/dot_general | solution.py:20
  322.6 6.4 %convolution_convert_fusion = bf16[2048,2048]{1,0:T(8,128)(2,1)S(1)} fusion(bf16[1,1,2048,512]{2,3,1,0:T(8,128)(2,1)S(1)} %fusion.68, bf16[1,2048,512]{2,1,0:T(8,128)(2,1)} %all-gather.33.cloned.1.call-done), kind=kOutput, calls=%fused_computation.41 | convolution fusion | flops 4299161600 | bytes 12582912 | tf_op jit(solution)/vmap(transpose(jvp()))/dot_general | solution.py:9
  329.0 3.2 copy-done.6
  332.3 15.8 %fusion.7 = bf16[2048,2048]{1,0:T(8,128)(2,1)} fusion(f32[2048,2048]{1,0:T(8,128)} %fusion.87, f32[2048,2048]{1,0:T(8,128)} %fusion.84, bf16[2048,2048]{1,0:T(8,128)(2,1)S(1)} %convolution_convert_fusion), kind=kLoop, calls=%fused_computation.13 | loop fusion | flops 50331648 | bytes 50331648
  348.5 11.7 %fusion.55 = bf16[2048,512]{0,1:T(8,128)(2,1)S(1)} fusion(bf16[2048,2048]{1,0:T(8,128)(2,1)} %copy-done.6, f32[2048,2048]{1,0:T(8,128)} %fusion.87, bf16[1,512,2048]{2,1,0:T(8,128)(2,1)} %all-gather.31.cloned.1.call-done), kind=kOutput, calls=%fused_computation.73 | convolution fusion | flops 4321181696 | bytes 29360128 | tf_op jit(solution)/vmap(transpose(jvp()))/dot_general | solution.py:21
  360.7 6.0 fusion.38
  366.7 6.1 convolution_bitcast_fusion
  372.9 13.2 %fusion.46 = f32[1,512,2048]{2,1,0:T(8,128)} fusion(bf16[2048,2048]{1,0:T(8,128)(2,1)} %convolution_convert_fusion.1, f32[2048,2048]{1,0:T(8,128)} %fusion.79, bf16[1,1,2048,512]{2,3,1,0:T(8,128)(2,1)} %get-tuple-element.15, f32[2048]{0:T(1024)S(1)} %bitcast.270), kind=kOutput, calls=%fused_computation.69 | convolution fusion | flops 4323278848 | bytes 31465472 | tf_op jit(solution)/vmap(transpose(jvp()))/dot_general | solution.py:21
  386.5 12.6 %fusion.49 = f32[1,512,2048]{2,1,0:T(8,128)} fusion(bf16[2048,2048]{1,0:T(8,128)(2,1)} %copy-done.6, f32[2048,2048]{1,0:T(8,128)} %fusion.87, bf16[1,2048,512]{1,2,0:T(8,128)(2,1)S(1)} %copy-done.4, f32[2048]{0:T(1024)S(1)} %bitcast.272), kind=kOutput, calls=%fused_computation.70 | convolution fusion | flops 4323278848 | bytes 31465472 | tf_op jit(solution)/vmap(transpose(jvp()))/dot_general | solution.py:21
  399.1 4.9 fusion.67
  404.1 3.9 copy.2
  408.0 1.1 convert_bitcast_fusion
  409.1 1.1 convert_bitcast_fusion.1
  410.2 0.8 add_bitcast_fusion
  411.0 41.6 %reduce-scatter.19.cloned.1.call-done = f32[1,64,2048]{2,1,0:T(8,128)} async-done(((f32[1,512,2048]{2,1,0:T(8,128)}), f32[1,64,2048]{2,1,0:T(8,128)}) %reduce-scatter.19.cloned.1.call-update) | async-done | bytes 524304
  452.6 1.1 convert_bitcast_fusion.5
  453.7 51.9 %reduce-scatter.21.cloned.1.call-done = f32[1,64,2048]{2,1,0:T(8,128)} async-done(((f32[1,512,2048]{2,1,0:T(8,128)}), f32[1,64,2048]{2,1,0:T(8,128)}) %reduce-scatter.21.cloned.1.call-update) | async-done | bytes 524304
  505.6 1.1 convert_bitcast_fusion.4
  506.7 0.8 add_bitcast_fusion.2
  507.5 51.2 %reduce-scatter.23.cloned.1.call-done = f32[1,64,2048]{2,1,0:T(8,128)} async-done(((f32[1,512,2048]{2,1,0:T(8,128)}), f32[1,64,2048]{2,1,0:T(8,128)}) %reduce-scatter.23.cloned.1.call-update) | async-done | bytes 524304
  558.7 1.1 convert_bitcast_fusion.3
  559.8 51.9 %reduce-scatter.25.cloned.1.call-done = f32[1,64,2048]{2,1,0:T(8,128)} async-done(((f32[1,512,2048]{2,1,0:T(8,128)}), f32[1,64,2048]{2,1,0:T(8,128)}) %reduce-scatter.25.cloned.1.call-update) | async-done | bytes 524304
  611.6 1.1 convert_bitcast_fusion.2
  612.7 0.8 add_bitcast_fusion.1
  (57 shorter events, 5.3 us)
Async XLA Ops:
  7.2 8.1 %copy-start.2 = (bf16[1,2048,512]{2,1,0:T(8,128)(2,1)S(1)}, bf16[1,2048,512]{2,1,0:T(8,128)(2,1)}, u32[]{:S(2)}) copy-start(bf16[1,2048,512]{2,1,0:T(8,128)(2,1)} %param.1) | copy-start | bytes 6291460
  7.2 43.6 %all-gather.29.cloned.1.call-start = ((), (), s32[]{:S(2)}) async-start(), calls=%async_computation.6 | async-start | bytes 2359296 | tf_op jit(solution)/vmap(jvp())/squeeze | solution.py:27
  9.3 79.5 %all-gather.31.cloned.1.call-start = ((), (), s32[]{:S(2)}) async-start(), calls=%async_computation.7 | async-start | bytes 2359296 | tf_op jit(solution)/vmap(jvp())/squeeze | solution.py:27
  11.3 114.9 %all-gather.33.cloned.1.call-start = ((), (), s32[]{:S(2)}) async-start(), calls=%async_computation.8 | async-start | bytes 2359296 | tf_op jit(solution)/vmap(jvp())/squeeze | solution.py:27
  13.3 150.2 %all-gather.37.cloned.1.call-start = ((), (), s32[]{:S(2)}) async-start(), calls=%async_computation.10 | async-start | bytes 2359296 | tf_op jit(solution)/vmap(jvp())/squeeze | solution.py:27
  14.0 187.4 %all-gather.35.cloned.1.call-start = ((), (), s32[]{:S(2)}) async-start(), calls=%async_computation.9 | async-start | bytes 2359296 | tf_op jit(solution)/vmap(jvp())/squeeze | solution.py:27
  14.6 224.7 %all-gather.39.cloned.1.call-start = ((), (), s32[]{:S(2)}) async-start(), calls=%async_computation.11 | async-start | bytes 2359296 | tf_op jit(solution)/vmap(jvp())/squeeze | solution.py:27
  15.2 392.7 %reduce-scatter.29.cloned.1.call-start = ((), (), s32[]{:S(2)}) async-start(), calls=%async_computation.17 | async-start | bytes 4718592
  88.8 11.0 %copy-start = (f32[2048,2048]{1,0:T(8,128)S(1)}, f32[2048,2048]{1,0:T(8,128)}, u32[]{:S(2)}) copy-start(f32[2048,2048]{1,0:T(8,128)} %fusion.87) | copy-start | bytes 50331652
  99.8 26.5 %copy-start.3 = (bf16[1,2048,512]{1,2,0:T(8,128)(2,1)S(1)}, bf16[1,2048,512]{1,2,0:T(8,128)(2,1)}, u32[]{:S(2)}) copy-start(bf16[1,2048,512]{1,2,0:T(8,128)(2,1)} %copy.1) | copy-start | bytes 6291460
  136.5 64.9 %copy-start.9 = (bf16[1,1,2048,512]{2,3,1,0:T(8,128)(2,1)S(1)}, bf16[1,1,2048,512]{2,3,1,0:T(8,128)(2,1)}, u32[]{:S(2)}) copy-start(bf16[1,1,2048,512]{2,3,1,0:T(8,128)(2,1)} %get-tuple-element.15) | copy-start | bytes 6291460
  239.3 10.9 %copy-start.1 = (f32[2048,2048]{1,0:T(8,128)S(1)}, f32[2048,2048]{1,0:T(8,128)}, u32[]{:S(2)}) copy-start(f32[2048,2048]{1,0:T(8,128)} %fusion.79) | copy-start | bytes 50331652
  274.4 9.6 %copy-start.5 = (bf16[1,2048,512]{1,2,0:T(8,128)(2,1)S(1)}, bf16[1,2048,512]{1,2,0:T(8,128)(2,1)}, u32[]{:S(2)}) copy-start(bf16[1,2048,512]{1,2,0:T(8,128)(2,1)} %copy) | copy-start | bytes 6291460
  274.4 9.6 %copy-start.10 = (bf16[1,1,2048,512]{2,3,1,0:T(8,128)(2,1)S(1)}, bf16[1,1,2048,512]{2,3,1,0:T(8,128)(2,1)}, u32[]{:S(2)}) copy-start(bf16[1,1,2048,512]{2,3,1,0:T(8,128)(2,1)} %get-tuple-element.15) | copy-start | bytes 6291460
  285.5 37.1 %copy-start.8 = (bf16[1,1,2048,512]{2,3,1,0:T(8,128)(2,1)}, bf16[1,1,2048,512]{2,3,1,0:T(8,128)(2,1)S(1)}, u32[]{:S(2)}) copy-start(bf16[1,1,2048,512]{2,3,1,0:T(8,128)(2,1)S(1)} %fusion.68) | copy-start | bytes 6291460
  296.0 113.0 %reduce-scatter.27.cloned.1.call-start = ((), (), s32[]{:S(2)}) async-start(), calls=%async_computation.16 | async-start | bytes 4718592
  311.9 140.8 %reduce-scatter.19.cloned.1.call-start = ((), (), s32[]{:S(2)}) async-start(), calls=%async_computation.12 | async-start | bytes 4718592
  329.0 3.2 copy-start.6
  348.2 12.1 %copy-start.4 = (bf16[1,2048,512]{1,2,0:T(8,128)(2,1)S(1)}, bf16[1,2048,512]{1,2,0:T(8,128)(2,1)}, u32[]{:S(2)}) copy-start(bf16[1,2048,512]{1,2,0:T(8,128)(2,1)} %copy.1) | copy-start | bytes 6291460
  348.2 157.4 %reduce-scatter.21.cloned.1.call-start = ((), (), s32[]{:S(2)}) async-start(), calls=%async_computation.13 | async-start | bytes 4718592
  348.5 11.8 %copy-start.7 = (bf16[2048,2048]{1,0:T(8,128)(2,1)S(1)}, bf16[2048,2048]{1,0:T(8,128)(2,1)}, u32[]{:S(2)}) copy-start(bf16[2048,2048]{1,0:T(8,128)(2,1)} %fusion.7) | copy-start | bytes 25165828
  348.5 12.2 %copy-start.12 = (bf16[1,512,2048]{2,1,0:T(8,128)(2,1)S(1)}, bf16[1,512,2048]{2,1,0:T(8,128)(2,1)}, u32[]{:S(2)}) copy-start(bf16[1,512,2048]{2,1,0:T(8,128)(2,1)} %all-gather.29.cloned.1.call-done) | copy-start | bytes 6291460
  360.7 6.0 copy-start.11
  372.9 185.8 %reduce-scatter.23.cloned.1.call-start = ((), (), s32[]{:S(2)}) async-start(), calls=%async_computation.14 | async-start | bytes 4718592
  386.2 225.5 %reduce-scatter.25.cloned.1.call-start = ((), (), s32[]{:S(2)}) async-start(), calls=%async_computation.15 | async-start | bytes 4718592
Sparse Core Ops, SparseCore 0:
  9.6 41.1 all-gather.28
  53.0 35.8 all-gather.30
  90.4 35.8 all-gather.32
  127.7 35.8 all-gather.36
  165.5 35.8 all-gather.34
  203.4 35.8 all-gather.38
  296.2 50.2 reduce-scatter.28
  348.8 50.6 reduce-scatter.26
  401.9 50.7 reduce-scatter.18
  454.8 50.7 reduce-scatter.20
  507.9 50.7 reduce-scatter.22
  560.9 50.7 reduce-scatter.24
where the time goes:
time: 627 us; the launch traced here: 621 us
  waiting for transfers between devices  353 us (56%)
  matrix products  174 us (28%)
  other arithmetic  57.6 us (9%)
  local copies, waits for them, and re-layouts  19.7 us (3%)
  between operations  14.7 us (2%)
    unnamed x18, waiting for transfers between devices  199 us
    squeeze x6, waiting for transfers between devices, stack(): h = layer(h, {name: w[number] for name, w in weights.items()})  155 us
    dot_general x6, matrix products, layer(): up = jnp.dot(a, w['w_up'], preferred_element_type=jnp.float32)  69.6 us
    dot_general x5, matrix products, matmul(): jnp.dot(a, w, preferred_element_type=jnp.float32).astype(jnp.bfloat16)  52.8 us
    dot_general x6, matrix products, layer(): gate = jnp.dot(a, w['w_gate'], preferred_element_type=jnp.float32)  51.5 us
    unnamed x3, other arithmetic  41.2 us
    unnamed x29, local copies, waits for them, and re-layouts  14 us
  transfers between devices with their start and end apart: 12, of which 10 were waited for; matrix products, arithmetic and copies ran while one was open for 30% of the time, Pallas kernels for 0%

commit v1 on v0

v1 whole, which is shorter than its diff:
```python
import functools

import jax
import jax.numpy as jnp
from jax import lax
from jax.experimental import pallas as pl
from jax.experimental.pallas import tpu as pltpu
from jax.sharding import PartitionSpec as P

MESH = pl.DeviceIdType.MESH
F32, BF16 = jnp.float32, jnp.bfloat16
SEGMENTS = 2
SLOTS = 5
RECV = 4
SEND = 2


def dot(a, b):
    return jnp.dot(a, b, preferred_element_type=F32)


def dot_nt(a, b):
    return lax.dot_general(a, b, (((1,), (1,)), ((), ())), preferred_element_type=F32)


def kernel(
    n, x_ref, dy_ref, wg_ref, wu_ref, wd_ref, dx_ref, dwg_ref, dwu_ref, dwd_ref,
    wgu, wdn, h, g, gt, a, at, act, dgu, da, term, sbuf, rbuf, outg, outu, outd,
    load_sem, ag_send, ag_recv, sw_send, sw_recv, rs_send, rs_recv,
):
    layers, _, d_model, ff = wgu.shape
    tokens = h.shape[1]
    rows = d_model // n
    drows = ff // n
    chunk = d_model // 2
    chunks = ff // chunk
    subs = drows // rows
    half = n // 2
    per_layer = subs + chunks
    units = layers * per_layer
    dbase = SLOTS * d_model
    seg = ff // SEGMENTS

    me, rep = lax.axis_index("dp"), lax.axis_index("rep")
    left, right = lax.rem(me + n - 1, n), lax.rem(me + 1, n)
    core = lax.rem(rep, 2)
    partner = rep + 1 - 2 * core
    toward = ({"dp": left}, {"dp": right})

    def at_distance(direction, k):
        return lax.rem(me + (n - k if direction == 0 else k), n)

    mine = pl.multiple_of(me * rows, rows)
    dmine = pl.multiple_of(me * drows, drows)
    loads = [pltpu.make_async_copy(x_ref.at[0], h.at[0], load_sem.at[0])]
    for l in range(layers):
        loads += [
            pltpu.make_async_copy(wg_ref.at[l], wgu.at[l, 0, pl.ds(mine, rows), :], load_sem.at[1 + 3 * l]),
            pltpu.make_async_copy(wu_ref.at[l], wgu.at[l, 1, pl.ds(mine, rows), :], load_sem.at[2 + 3 * l]),
            pltpu.make_async_copy(wd_ref.at[l], wdn.at[l, pl.ds(dmine, drows), :], load_sem.at[3 + 3 * l]),
        ]
    loads.append(pltpu.make_async_copy(dy_ref.at[0], g, load_sem.at[1 + 3 * layers]))
    for c in loads:
        c.start()

    barrier = pltpu.get_barrier_semaphore()
    for other in (*toward, {"rep": partner}):
        pl.semaphore_signal(barrier, inc=1, device_id=other, device_id_type=MESH)
    pl.semaphore_wait(barrier, 3)

    def piece(unit, origin, member, part=None):
        l, s = unit // (SEGMENTS + 1), unit % (SEGMENTS + 1)
        if s < SEGMENTS:
            size, first, width = rows // 2, s * seg, seg
            if part is not None:
                width = seg // 2
                first += part * width
            row = pl.multiple_of(origin * rows + member * size, size)
            return wgu.at[l, :, pl.ds(row, size), pl.ds(first, width)]
        size = drows // 2
        row = origin * drows + member * size
        if part is not None:
            size //= 2
            row += part * size
        return wdn.at[l, pl.ds(pl.multiple_of(row, size), size), :]

    def hop(unit, direction, k):
        origin = at_distance(1 - direction, k)
        ref = piece(unit, origin, core, direction if k == half - 1 else None)
        return pltpu.make_async_remote_copy(
            ref, ref, ag_send.at[unit, direction, k], ag_recv.at[unit, direction, k],
            device_id=toward[direction], device_id_type=MESH,
        )

    def landed(unit, direction, k):
        origin = at_distance(1 - direction, k + 1)
        ref = piece(unit, origin, core, direction if k == half - 1 else None)
        return pltpu.make_async_remote_copy(
            ref, ref, ag_send.at[unit, direction, k], ag_recv.at[unit, direction, k],
            device_id=toward[direction], device_id_type=MESH,
        )

    def swap(unit, direction, k, member):
        origin = at_distance(1 - direction, k + 1)
        ref = piece(unit, origin, member, direction if k == half - 1 else None)
        return pltpu.make_async_remote_copy(
            ref, ref, sw_send.at[unit, direction, k], sw_recv.at[unit, direction, k],
            device_id={"rep": partner}, device_id_type=MESH,
        )

    def gather(unit, k):
        for direction in range(2):
            if k > 0:
                landed(unit, direction, k - 1).wait_recv()
            if k < half:
                hop(unit, direction, k).start()
            if k > 0:
                swap(unit, direction, k - 1, core).start()

    def gathered(unit):
        for k in range(half):
            for direction in range(2):
                swap(unit, direction, k, 1 - core).wait_recv()

    def close(unit):
        for k in range(half):
            for direction in range(2):
                hop(unit, direction, k).wait_send()
                swap(unit, direction, k, core).wait_send()

    def place(u):
        step, v = u // per_layer, lax.rem(u, per_layer)
        l = layers - 1 - step
        mixed = 2 * subs - 1
        early = v < mixed
        down = early & ((v == 0) | (lax.rem(v, 2) == 1))
        index = jnp.where(down, (v + 1) // 2, jnp.where(early, v // 2 - 1, v - subs))
        slot = lax.rem(step * chunks + index, SLOTS)
        base = jnp.where(down, dbase + l * ff + index * rows, slot * d_model)
        stride = jnp.where(down, drows, rows)
        return l, down, index, base, stride

    def rs_copy(direction, k, u):
        lo, size = (direction * (rows // 2), rows // 2) if k == 0 else (0, rows)
        return pltpu.make_async_remote_copy(
            sbuf.at[direction, k, lax.rem(u, SEND), pl.ds(lo, size), :],
            rbuf.at[direction, k, lax.rem(u, RECV), pl.ds(lo, size), :],
            rs_send.at[direction, k, lax.rem(u, SEND)],
            rs_recv.at[direction, k, lax.rem(u, RECV)],
            device_id=toward[direction],
            device_id_type=MESH,
        )

    def stage(t, k):
        u = t - k
        l, down, index, base, stride = place(u)
        hrows = rows // 2

        def own(owner, lo, size):
            return term[pl.ds(pl.multiple_of(base + owner * stride + lo, hrows), size), :]

        if k == half:
            for direction in range(2):
                rs_copy(direction, half - 1, u).wait_recv()
            slot = lax.rem(u, RECV)
            total = own(me, 0, rows)
            for direction in range(2):
                total += rbuf[direction, half - 1, slot].astype(F32)
            total = total.astype(BF16)

            @pl.when(down)
            def _():
                outd[l, pl.ds(pl.multiple_of(index * rows, rows), rows), :] = total

            @pl.when(jnp.logical_not(down))
            def _():
                columns = pl.ds(pl.multiple_of(index * chunk, chunk), chunk)
                outg[l, :, columns] = total[:, :chunk]
                outu[l, :, columns] = total[:, chunk:]

            return
        for direction in range(2):

            @pl.when(u >= SEND)
            def _():
                rs_copy(direction, k, u - SEND).wait_send()

            owner = at_distance(direction, half - k)
            to = sbuf.at[direction, k, lax.rem(u, SEND)]
            lo = direction * hrows
            if k == 0:
                to[pl.ds(lo, hrows), :] = own(owner, lo, hrows).astype(BF16)
            else:
                rs_copy(direction, k - 1, u).wait_recv()
                came = rbuf.at[direction, k - 1, lax.rem(u, RECV)]
                if k == 1:
                    rest = hrows - lo
                    to[pl.ds(lo, hrows), :] = (own(owner, lo, hrows) + came[pl.ds(lo, hrows), :].astype(F32)).astype(BF16)
                    to[pl.ds(rest, hrows), :] = own(owner, rest, hrows).astype(BF16)
                else:
                    to[...] = (own(owner, 0, rows) + came[...].astype(F32)).astype(BF16)
            rs_copy(direction, k, u).start()

    def tick(t):
        for k in range(half + 1):
            pl.when((t >= k) & (t - k < units))(functools.partial(stage, t, k))

    small, tile = min(256, tokens), min(512, tokens)

    def normed(l):
        @pl.loop(0, tokens // small)
        def _(i):
            ts = pl.ds(pl.multiple_of(i * small, small), small)
            wide = h[l, ts, :].astype(F32)
            scale = lax.rsqrt(jnp.mean(wide * wide, -1, keepdims=True) + 1e-6)
            rounded = (wide * scale).astype(BF16)
            a[ts, :] = rounded
            at[:, ts] = rounded.T

    def turn():
        @pl.loop(0, tokens // small)
        def _(i):
            ts = pl.ds(pl.multiple_of(i * small, small), small)
            gt[:, ts] = g[ts, :].T

    def gate_up(l, ts, columns):
        rows_in = a[ts, :]
        return dot(rows_in, wgu[l, 0, :, columns]), dot(rows_in, wgu[l, 1, :, columns])

    def forward(l, s):
        tiles = tokens // tile

        @pl.loop(0, seg // chunk * tiles)
        def _(i):
            columns = pl.ds(pl.multiple_of(s * seg + i // tiles * chunk, chunk), chunk)
            ts = pl.ds(pl.multiple_of(lax.rem(i, tiles) * tile, tile), tile)
            gate, up = gate_up(l, ts, columns)
            act[ts, columns] = (gate * jax.nn.sigmoid(gate) * up).astype(BF16)

    def down_forward(l):
        @pl.loop(0, tokens // small)
        def _(i):
            ts = pl.ds(pl.multiple_of(i * small, small), small)
            out = dot(act[ts, :], wdn[l]).astype(BF16)
            h[l + 1, ts, :] = (h[l, ts, :].astype(F32) + out.astype(F32)).astype(BF16)

    def down_gradient(l):
        @pl.loop(0, chunks)
        def _(j):
            columns = pl.ds(pl.multiple_of(j * chunk, chunk), chunk)
            out = dot(gt[...], act[:, columns])
            term[pl.ds(pl.multiple_of(dbase + l * ff + j * chunk, chunk), chunk), :] = out.T

    def backward_tokens(l, j):
        columns = pl.ds(pl.multiple_of(j * chunk, chunk), chunk)

        @pl.loop(0, tokens // tile)
        def _(i):
            ts = pl.ds(pl.multiple_of(i * tile, tile), tile)
            gate, up = gate_up(l, ts, columns)
            by_act = dot_nt(g[ts, :], wdn[l, columns, :]).astype(BF16).astype(F32)
            sig = jax.nn.sigmoid(gate)
            silu = gate * sig
            by_up = (by_act * silu).astype(BF16)
            by_gate = (by_act * up * (sig + silu * (1.0 - sig))).astype(BF16)
            dgu[ts, :chunk] = by_gate
            dgu[ts, chunk:] = by_up
            by_a = dot_nt(by_gate, wgu[l, 0, :, columns]) + dot_nt(by_up, wgu[l, 1, :, columns])

            @pl.when(j == 0)
            def _():
                da[ts, :] = by_a

            @pl.when(j > 0)
            def _():
                da[ts, :] += by_a

    def gate_up_gradient(step, j):
        row = pl.multiple_of(lax.rem(step * chunks + j, SLOTS) * d_model, d_model)

        @pl.loop(0, 2)
        def _(i):
            columns = pl.ds(pl.multiple_of(i * chunk, chunk), chunk)
            term[pl.ds(row, d_model), columns] = dot(at[...], dgu[:, columns])

    def norm_backward(l):
        @pl.loop(0, tokens // small)
        def _(i):
            ts = pl.ds(pl.multiple_of(i * small, small), small)
            by_a = da[ts, :].astype(BF16).astype(F32)
            wide = h[l, ts, :].astype(F32)
            scale = lax.rsqrt(jnp.mean(wide * wide, -1, keepdims=True) + 1e-6)
            by_scale = jnp.sum(by_a * wide, -1, keepdims=True)
            by_wide = by_a * scale - (by_scale * scale / d_model) * (scale * scale) * wide
            g[ts, :] = (g[ts, :].astype(F32) + by_wide.astype(BF16).astype(F32)).astype(BF16)

    per = SEGMENTS + 1
    for c in loads[1:4]:
        c.wait()
    for unit in range(per):
        gather(unit, 0)
    loads[0].wait()
    normed(0)
    for k in range(1, half):
        for unit in range(per):
            gather(unit, k)
    for c in loads[4:]:
        c.wait()
    for l in range(layers):
        for s in range(SEGMENTS):
            unit = l * per + s
            gather(unit, half)
            if l + 1 < layers:
                for later in range(unit + per - s, unit + 2 * per - s):
                    gather(later, s)
            gathered(unit)
            forward(l, s)
        unit = l * per + SEGMENTS
        gather(unit, half)
        gathered(unit)
        if l + 1 < layers:
            for k in range(SEGMENTS, half):
                for later in range(unit + 1, unit + 1 + per):
                    gather(later, k)
                if k == SEGMENTS:
                    down_forward(l)
            normed(l + 1)

    for step, l in enumerate(reversed(range(layers))):
        turn()
        if step > 0:
            normed(l)
        if step > 0:
            for s in range(SEGMENTS):
                forward(l, s)
        down_gradient(l)
        start = step * per_layer
        tick(start)

        @pl.loop(0, chunks)
        def _(j):
            backward_tokens(l, j)

            @pl.when(j < subs - 1)
            def _():
                tick(start + 1 + 2 * j)

            gate_up_gradient(step, j)
            tick(start + jnp.where(j < subs - 1, 2 + 2 * j, j + subs))

        norm_backward(l)

    out_dx = pltpu.make_async_copy(g, dx_ref.at[0], load_sem.at[0])
    out_dx.start()

    @pl.loop(0, half)
    def _(i):
        tick(units + i)

    outs = [
        pltpu.make_async_copy(outg, dwg_ref, load_sem.at[1]),
        pltpu.make_async_copy(outu, dwu_ref, load_sem.at[2]),
        pltpu.make_async_copy(outd, dwd_ref, load_sem.at[3]),
    ]
    for c in outs:
        c.start()
    for direction in range(2):
        for k in range(half):
            for u in range(units - SEND, units):
                rs_copy(direction, k, u).wait_send()
    for unit in range(layers * per):
        close(unit)
    for c in (out_dx, *outs):
        c.wait()


def solution(mesh):
    n = mesh.shape["dp"]

    def step(x, dy, wg, wu, wd):
        _, tokens, d_model = x.shape
        layers, rows, ff = wg.shape
        drows = wd.shape[1]
        chunk = d_model // 2
        half = n // 2
        gather_units = layers * (SEGMENTS + 1)
        any_space = pl.BlockSpec(memory_space=pl.ANY)
        dma = pltpu.SemaphoreType.DMA
        return pl.pallas_call(
            functools.partial(kernel, n),
            out_shape=[jax.ShapeDtypeStruct(t.shape, t.dtype) for t in (x, wg, wu, wd)],
            in_specs=[any_space] * 5,
            out_specs=[any_space] * 4,
            scratch_shapes=[
                pltpu.VMEM((layers, 2, d_model, ff), BF16),
                pltpu.VMEM((layers, ff, d_model), BF16),
                pltpu.VMEM((layers, tokens, d_model), BF16),
                pltpu.VMEM((tokens, d_model), BF16),
                pltpu.VMEM((d_model, tokens), BF16),
                pltpu.VMEM((tokens, d_model), BF16),
                pltpu.VMEM((d_model, tokens), BF16),
                pltpu.VMEM((tokens, ff), BF16),
                pltpu.VMEM((tokens, 2 * chunk), BF16),
                pltpu.VMEM((tokens, d_model), F32),
                pltpu.VMEM((SLOTS * d_model + layers * ff, d_model), F32),
                pltpu.VMEM((2, half, SEND, rows, d_model), BF16),
                pltpu.VMEM((2, half, RECV, rows, d_model), BF16),
                pltpu.VMEM((layers, rows, ff), BF16),
                pltpu.VMEM((layers, rows, ff), BF16),
                pltpu.VMEM((layers, drows, d_model), BF16),
                dma((2 + 3 * layers,)),
                dma((gather_units, 2, half)),
                dma((gather_units, 2, half)),
                dma((gather_units, 2, half)),
                dma((gather_units, 2, half)),
                dma((2, half, SEND)),
                dma((2, half, RECV)),
            ],
            compiler_params=pltpu.CompilerParams(
                collective_id=0, has_side_effects=True, vmem_limit_bytes=67043328
            ),
        )(x, dy, wg, wu, wd)

    tokens_spec, weight_spec = P(("rep", "dp"), None, None), P(None, "dp", None)
    grad_spec = P("rep", "dp", None)
    return jax.shard_map(
        step,
        mesh=mesh,
        in_specs=(tokens_spec, tokens_spec, weight_spec, weight_spec, weight_spec),
        out_specs=(tokens_spec, grad_spec, grad_spec, grad_spec),
        check_vma=False,
    )
```

time: 627 us -> 296 us (0.47); the launches traced: 621 us -> 296 us
  waiting for transfers between devices: 353 us -> 0 us
  Pallas kernels: 0 us -> 290 us
  matrix products: 174 us -> 0 us
  other arithmetic: 57.6 us -> 0 us
  local copies, waits for them, and re-layouts: 19.7 us -> 5.52 us
  between operations: 14.7 us -> 0.66 us
    pallas_call x0 -> x1, Pallas kernels: none -> 290 us  [step(): pl.pallas_call(functools.partial(kernel, n), out_shape=[jax.ShapeDtypeStr...]
    unnamed x18 -> x0, waiting for transfers between devices: 199 us -> none
    dot_general x17 -> x0, matrix products: 174 us -> none  [the longest x6 69.6 us: layer(): up = jnp.dot(a, w['w_up'], preferred_element_type=jnp.float32)]
    squeeze x6 -> x0, waiting for transfers between devices: 155 us -> none  [stack(): h = layer(h, {name: w[number] for name, w in weights.items()})]
    unnamed x3 -> x0, other arithmetic: 41.2 us -> none
    unnamed x29 -> x10, local copies, waits for them, and re-layouts: 14 us -> 5.52 us
    reshape x4 -> x0, other arithmetic: 7.41 us -> none  [the longest x1 4.92 us: step(): by_x.reshape(shape)]
    broadcast_in_dim x6 -> x0, other arithmetic: 6.42 us -> none  [stack(): h = layer(h, {name: w[number] for name, w in weights.items()})]
  transfers between devices with their start and end apart: 12 -> 0, of which waited for: 10 -> 0; matrix products, arithmetic and copies ran while one was open for 30% -> 0% of each run, Pallas kernels for 0% -> 0%
where the time goes in v1:
time: 296 us
  Pallas kernels  290 us (98%)
  local copies, waits for them, and re-layouts  5.52 us (2%)
    pallas_call x1, Pallas kernels, step(): pl.pallas_call(functools.partial(kernel, n), out_shape=[jax.ShapeDtypeStr...  290 us

profile of v1, /device:TPU:28, one launch (start us, length us, event | category | flops | bytes accessed | tf_op | source)
XLA Modules:
  0.0 296.3 jit_solution(17828807366526302549)
XLA Ops:
  0.6 290.1 %shard_map.84 = (bf16[1,2048,512]{2,1,0:T(8,128)(2,1)}, bf16[2,64,2048]{2,1,0:T(8,128)(2,1)}, bf16[2,64,2048]{2,1,0:T(8,128)(2,1)}, bf16[2,256,512]{2,1,0:T(8,128)(2,1)}) custom-call(bf16[1,2048,512]{2,1,0:T(8,128)(2,1)} %x_ref.1, bf16[1,2048,512]{2,1,0:T(8,128)(2,1)} %dy_ref.1, bf16[2,64,2048]{2,1,0:T(8,128)(2,1)} %wg_ref.1, bf16[2,64,2048]{2,1,0:T(8,128)(2,1)} %wu_ref.1, ...), custom_call_target="tpu_custom_call" | custom-call | tf_op jit(solution)/shard_map/pallas_call | solution.py:389
  290.8 0.0 copy-start.2
  290.8 0.0 copy-start.1
  290.8 3.1 %copy.13 = bf16[1,2048,512]{2,1,0:T(8,128)(2,1)} copy(bf16[1,2048,512]{2,1,0:T(8,128)(2,1)} %get-tuple-element.8) | data formatting | bytes 4194304
  293.9 0.0 copy-done.2
  293.9 0.0 copy-start
  293.9 0.8 copy.14
  294.7 0.0 copy-done.1
  294.7 0.8 copy.15
  295.5 0.0 copy-done
  295.5 0.8 copy.16
Async XLA Ops:
  290.8 3.2 %copy-start.2 = (bf16[2,64,2048]{2,1,0:T(8,128)(2,1)S(1)}, bf16[2,64,2048]{2,1,0:T(8,128)(2,1)}, u32[]{:S(2)}) copy-start(bf16[2,64,2048]{2,1,0:T(8,128)(2,1)} %get-tuple-element.9) | copy-start | bytes 1572868
  290.8 3.9 %copy-start.1 = (bf16[2,64,2048]{2,1,0:T(8,128)(2,1)S(1)}, bf16[2,64,2048]{2,1,0:T(8,128)(2,1)}, u32[]{:S(2)}) copy-start(bf16[2,64,2048]{2,1,0:T(8,128)(2,1)} %get-tuple-element.10) | copy-start | bytes 1572868
  293.9 1.6 copy-start

commit v2 on v1

--- a/solution.py
+++ b/solution.py
@@ -11,8 +11,9 @@
 F32, BF16 = jnp.float32, jnp.bfloat16
 SEGMENTS = 2
 SLOTS = 5
-RECV = 4
-SEND = 2
+RECV = 8
+SEND = 3
+LAG = 2
 
 
 def dot(a, b):
@@ -24,9 +25,9 @@
 
 
 def kernel(
-    n, x_ref, dy_ref, wg_ref, wu_ref, wd_ref, dx_ref, dwg_ref, dwu_ref, dwd_ref,
+    n, x_ref, dy_ref, wg_ref, wu_ref, wd_ref, dx_ref, dwg_ref, dwu_ref, dwd_ref, kept,
     wgu, wdn, h, g, gt, a, at, act, dgu, da, term, sbuf, rbuf, outg, outu, outd,
-    load_sem, ag_send, ag_recv, sw_send, sw_recv, rs_send, rs_recv,
+    load_sem, keep_sem, ag_send, ag_recv, sw_send, sw_recv, rs_send, rs_recv,
 ):
     layers, _, d_model, ff = wgu.shape
     tokens = h.shape[1]
@@ -36,8 +37,8 @@
     chunks = ff // chunk
     subs = drows // rows
     half = n // 2
-    per_layer = subs + chunks
-    units = layers * per_layer
+    early = 2
+    per_layer = 1 + 2 * chunks + subs - early
     dbase = SLOTS * d_model
     seg = ff // SEGMENTS
 
@@ -129,16 +130,20 @@
                 swap(unit, direction, k, core).wait_send()
 
     def place(u):
-        step, v = u // per_layer, lax.rem(u, per_layer)
+        step = jnp.minimum(u // per_layer, layers - 1)
+        v = u - step * per_layer
         l = layers - 1 - step
-        mixed = 2 * subs - 1
-        early = v < mixed
-        down = early & ((v == 0) | (lax.rem(v, 2) == 1))
-        index = jnp.where(down, (v + 1) // 2, jnp.where(early, v // 2 - 1, v - subs))
-        slot = lax.rem(step * chunks + index, SLOTS)
+        last = step == layers - 1
+        soon = jnp.where(last, subs, early)
+        odd = lax.rem(v, 2) == 1
+        held = v - 2 * chunks - 1
+        down = (v == 0) | (odd & (v < 2 * soon - 1)) | ((held >= 0) & jnp.logical_not(last))
+        gate = jnp.logical_not(odd) & (v > 0) & (held < 0)
+        index = jnp.where(down, jnp.where(held >= 0, held + early, (v + 1) // 2), v // 2 - 1)
+        slot = lax.rem(step * chunks + jnp.maximum(index, 0), SLOTS)
         base = jnp.where(down, dbase + l * ff + index * rows, slot * d_model)
         stride = jnp.where(down, drows, rows)
-        return l, down, index, base, stride
+        return down | gate, l, down, index, base, stride
 
     def rs_copy(direction, k, u):
         lo, size = (direction * (rows // 2), rows // 2) if k == 0 else (0, rows)
@@ -151,9 +156,7 @@
             device_id_type=MESH,
         )
 
-    def stage(t, k):
-        u = t - k
-        l, down, index, base, stride = place(u)
+    def stage(u, k, l, down, index, base, stride):
         hrows = rows // 2
 
         def own(owner, lo, size):
@@ -161,6 +164,7 @@
 
         if k == half:
             for direction in range(2):
+                rs_copy(direction, half - 1, u).wait_send()
                 rs_copy(direction, half - 1, u).wait_recv()
             slot = lax.rem(u, RECV)
             total = own(me, 0, rows)
@@ -180,17 +184,13 @@
 
             return
         for direction in range(2):
-
-            @pl.when(u >= SEND)
-            def _():
-                rs_copy(direction, k, u - SEND).wait_send()
-
             owner = at_distance(direction, half - k)
             to = sbuf.at[direction, k, lax.rem(u, SEND)]
             lo = direction * hrows
             if k == 0:
                 to[pl.ds(lo, hrows), :] = own(owner, lo, hrows).astype(BF16)
             else:
+                rs_copy(direction, k - 1, u).wait_send()
                 rs_copy(direction, k - 1, u).wait_recv()
                 came = rbuf.at[direction, k - 1, lax.rem(u, RECV)]
                 if k == 1:
@@ -203,7 +203,9 @@
 
     def tick(t):
         for k in range(half + 1):
-            pl.when((t >= k) & (t - k < units))(functools.partial(stage, t, k))
+            u = t - LAG * k
+            there, *rest = place(jnp.maximum(u, 0))
+            pl.when((u >= 0) & there)(functools.partial(stage, u, k, *rest))
 
     small, tile = min(256, tokens), min(512, tokens)
 
@@ -223,65 +225,70 @@
             ts = pl.ds(pl.multiple_of(i * small, small), small)
             gt[:, ts] = g[ts, :].T
 
-    def gate_up(l, ts, columns):
-        rows_in = a[ts, :]
-        return dot(rows_in, wgu[l, 0, :, columns]), dot(rows_in, wgu[l, 1, :, columns])
+    def both(l, columns):
+        return jnp.concatenate([wgu[l, 0, :, columns], wgu[l, 1, :, columns]], 1)
 
     def forward(l, s):
-        tiles = tokens // tile
-
-        @pl.loop(0, seg // chunk * tiles)
+        @pl.loop(0, seg // chunk)
+        def _(j):
+            columns = pl.ds(pl.multiple_of(s * seg + j * chunk, chunk), chunk)
+            w = both(l, columns)
+            for i in range(tokens // tile):
+                ts = pl.ds(i * tile, tile)
+                out = dot(a[ts, :], w)
+                gate, up = out[:, :chunk], out[:, chunk:]
+                act[ts, columns] = (gate * jax.nn.sigmoid(gate) * up).astype(BF16)
+
+    def down_forward(l):
+        part = 2 * tile if tokens % (2 * tile) == 0 else tile
+
+        @pl.loop(0, tokens // part)
         def _(i):
-            columns = pl.ds(pl.multiple_of(s * seg + i // tiles * chunk, chunk), chunk)
-            ts = pl.ds(pl.multiple_of(lax.rem(i, tiles) * tile, tile), tile)
-            gate, up = gate_up(l, ts, columns)
-            act[ts, columns] = (gate * jax.nn.sigmoid(gate) * up).astype(BF16)
-
-    def down_forward(l):
-        @pl.loop(0, tokens // small)
+            for p in range(part // tile):
+                ts = pl.ds(pl.multiple_of(i * part + p * tile, tile), tile)
+                out = dot(act[ts, :], wdn[l]).astype(BF16)
+                h[l + 1, ts, :] = (h[l, ts, :].astype(F32) + out.astype(F32)).astype(BF16)
+
+    def down_gradient(l):
+        @pl.loop(0, chunks // 2)
         def _(i):
-            ts = pl.ds(pl.multiple_of(i * small, small), small)
-            out = dot(act[ts, :], wdn[l]).astype(BF16)
-            h[l + 1, ts, :] = (h[l, ts, :].astype(F32) + out.astype(F32)).astype(BF16)
-
-    def down_gradient(l):
-        @pl.loop(0, chunks)
-        def _(j):
-            columns = pl.ds(pl.multiple_of(j * chunk, chunk), chunk)
-            out = dot(gt[...], act[:, columns])
-            term[pl.ds(pl.multiple_of(dbase + l * ff + j * chunk, chunk), chunk), :] = out.T
+            for p in range(2):
+                j = 2 * i + p
+                columns = pl.ds(pl.multiple_of(j * chunk, chunk), chunk)
+                out = dot(gt[...], act[:, columns])
+                term[pl.ds(pl.multiple_of(dbase + l * ff + j * chunk, chunk), chunk), :] = out.T
 
     def backward_tokens(l, j):
         columns = pl.ds(pl.multiple_of(j * chunk, chunk), chunk)
-
-        @pl.loop(0, tokens // tile)
-        def _(i):
-            ts = pl.ds(pl.multiple_of(i * tile, tile), tile)
-            gate, up = gate_up(l, ts, columns)
-            by_act = dot_nt(g[ts, :], wdn[l, columns, :]).astype(BF16).astype(F32)
+        w, w_down = both(l, columns), wdn[l, columns, :]
+
+        def first(i):
+            ts = pl.ds(i * tile, tile)
+            return dot(a[ts, :], w), dot_nt(g[ts, :], w_down)
+
+        def second(i, out, by_act):
+            ts = pl.ds(i * tile, tile)
+            gate, up = out[:, :chunk], out[:, chunk:]
+            by_act = by_act.astype(BF16).astype(F32)
             sig = jax.nn.sigmoid(gate)
             silu = gate * sig
             by_up = (by_act * silu).astype(BF16)
             by_gate = (by_act * up * (sig + silu * (1.0 - sig))).astype(BF16)
-            dgu[ts, :chunk] = by_gate
-            dgu[ts, chunk:] = by_up
-            by_a = dot_nt(by_gate, wgu[l, 0, :, columns]) + dot_nt(by_up, wgu[l, 1, :, columns])
-
-            @pl.when(j == 0)
-            def _():
-                da[ts, :] = by_a
-
-            @pl.when(j > 0)
-            def _():
-                da[ts, :] += by_a
+            by_both = jnp.concatenate([by_gate, by_up], 1)
+            dgu[ts, :] = by_both
+            da[ts, :] += dot_nt(by_both, w)
+
+        tiles = tokens // tile
+        ready = first(0)
+        for i in range(1, tiles):
+            after = first(i)
+            second(i - 1, *ready)
+            ready = after
+        second(tiles - 1, *ready)
 
     def gate_up_gradient(step, j):
         row = pl.multiple_of(lax.rem(step * chunks + j, SLOTS) * d_model, d_model)
-
-        @pl.loop(0, 2)
-        def _(i):
-            columns = pl.ds(pl.multiple_of(i * chunk, chunk), chunk)
-            term[pl.ds(row, d_model), columns] = dot(at[...], dgu[:, columns])
+        term[pl.ds(row, d_model), :] = dot(at[...], dgu[...])
 
     def norm_backward(l):
         @pl.loop(0, tokens // small)
@@ -306,7 +313,11 @@
             gather(unit, k)
     for c in loads[4:]:
         c.wait()
+    keeps = []
     for l in range(layers):
+        for c in keeps:
+            c.wait()
+        keeps = []
         for s in range(SEGMENTS):
             unit = l * per + s
             gather(unit, half)
@@ -315,6 +326,10 @@
                     gather(later, s)
             gathered(unit)
             forward(l, s)
+            if l + 1 < layers:
+                columns = pl.ds(s * seg, seg)
+                keeps.append(pltpu.make_async_copy(act.at[:, columns], kept.at[l, :, columns], keep_sem.at[s]))
+                keeps[-1].start()
         unit = l * per + SEGMENTS
         gather(unit, half)
         gathered(unit)
@@ -327,35 +342,37 @@
             normed(l + 1)
 
     for step, l in enumerate(reversed(range(layers))):
+        start = step * per_layer
         turn()
         if step > 0:
             normed(l)
-        if step > 0:
-            for s in range(SEGMENTS):
-                forward(l, s)
+            tick(start - 1)
+            back.wait()
+        da[...] = jnp.zeros_like(da)
         down_gradient(l)
-        start = step * per_layer
+        if l > 0:
+            back = pltpu.make_async_copy(kept.at[l - 1], act, keep_sem.at[SEGMENTS])
+            back.start()
         tick(start)
 
         @pl.loop(0, chunks)
         def _(j):
             backward_tokens(l, j)
-
-            @pl.when(j < subs - 1)
-            def _():
-                tick(start + 1 + 2 * j)
-
+            tick(start + 1 + 2 * j)
             gate_up_gradient(step, j)
-            tick(start + jnp.where(j < subs - 1, 2 + 2 * j, j + subs))
+            tick(start + 2 + 2 * j)
 
         norm_backward(l)
+        if l > 0:
+            for i in range(subs - early - 1):
+                tick(start + 1 + 2 * chunks + i)
 
     out_dx = pltpu.make_async_copy(g, dx_ref.at[0], load_sem.at[0])
     out_dx.start()
 
-    @pl.loop(0, half)
+    @pl.loop(0, LAG * half)
     def _(i):
-        tick(units + i)
+        tick((layers - 1) * per_layer + 2 * chunks + 1 + i)
 
     outs = [
         pltpu.make_async_copy(outg, dwg_ref, load_sem.at[1]),
@@ -364,10 +381,6 @@
     ]
     for c in outs:
         c.start()
-    for direction in range(2):
-        for k in range(half):
-            for u in range(units - SEND, units):
-                rs_copy(direction, k, u).wait_send()
     for unit in range(layers * per):
         close(unit)
     for c in (out_dx, *outs):
@@ -388,9 +401,12 @@
         dma = pltpu.SemaphoreType.DMA
         return pl.pallas_call(
             functools.partial(kernel, n),
-            out_shape=[jax.ShapeDtypeStruct(t.shape, t.dtype) for t in (x, wg, wu, wd)],
+            out_shape=[
+                *(jax.ShapeDtypeStruct(t.shape, t.dtype) for t in (x, wg, wu, wd)),
+                jax.ShapeDtypeStruct((layers - 1, tokens, ff), BF16),
+            ],
             in_specs=[any_space] * 5,
-            out_specs=[any_space] * 4,
+            out_specs=[any_space] * 5,
             scratch_shapes=[
                 pltpu.VMEM((layers, 2, d_model, ff), BF16),
                 pltpu.VMEM((layers, ff, d_model), BF16),
@@ -409,6 +425,7 @@
                 pltpu.VMEM((layers, rows, ff), BF16),
                 pltpu.VMEM((layers, drows, d_model), BF16),
                 dma((2 + 3 * layers,)),
+                dma((SEGMENTS + 1,)),
                 dma((gather_units, 2, half)),
                 dma((gather_units, 2, half)),
                 dma((gather_units, 2, half)),
@@ -419,7 +436,7 @@
             compiler_params=pltpu.CompilerParams(
                 collective_id=0, has_side_effects=True, vmem_limit_bytes=67043328
             ),
-        )(x, dy, wg, wu, wd)
+        )(x, dy, wg, wu, wd)[:4]
 
     tokens_spec, weight_spec = P(("rep", "dp"), None, None), P(None, "dp", None)
     grad_spec = P("rep", "dp", None)

time: 296 us -> 233 us (0.79)
  Pallas kernels: 290 us -> 227 us
    pallas_call x1, Pallas kernels: 290 us -> 227 us  [step(): pl.pallas_call(functools.partial(kernel, n), out_shape=[*(jax.ShapeDtypeS...]
where the time goes in v2:
time: 233 us
  Pallas kernels  227 us (97%)
  local copies, waits for them, and re-layouts  5.52 us (2%)
    pallas_call x1, Pallas kernels, step(): pl.pallas_call(functools.partial(kernel, n), out_shape=[*(jax.ShapeDtypeS...  227 us
    unnamed x10, local copies, waits for them, and re-layouts  5.52 us

profile of v2, /device:TPU:28, one launch (start us, length us, event | category | flops | bytes accessed | tf_op | source)
XLA Modules:
  0.0 233.0 jit_solution(16056796890777275932)
XLA Ops:
  0.6 226.8 %shard_map.84 = (bf16[1,2048,512]{2,1,0:T(8,128)(2,1)}, bf16[2,64,2048]{2,1,0:T(8,128)(2,1)}, bf16[2,64,2048]{2,1,0:T(8,128)(2,1)}, bf16[2,256,512]{2,1,0:T(8,128)(2,1)}, bf16[1,2048,2048]{2,1,0:T(8,128)(2,1)}) custom-call(bf16[1,2048,512]{2,1,0:T(8,128)(2,1)} %x_ref.1, bf16[1,2048,512]{2,1,0:T(8,128)(2,1)} %dy_ref.1, bf16[2,64,2048]{2,1,0:T(8,128)(2,1)} %wg_ref.1, ...), custom_call_target="tpu_custom_call" | custom-call | tf_op jit(solution)/shard_map/pallas_call | solution.py:402
  227.5 0.0 copy-start.2
  227.5 0.0 copy-start.1
  227.5 3.1 %copy.13 = bf16[1,2048,512]{2,1,0:T(8,128)(2,1)} copy(bf16[1,2048,512]{2,1,0:T(8,128)(2,1)} %get-tuple-element.16) | data formatting | bytes 4194304
  230.6 0.0 copy-done.2
  230.6 0.0 copy-start
  230.6 0.8 copy.14
  231.4 0.0 copy-done.1
  231.4 0.8 copy.15
  232.2 0.0 copy-done
  232.2 0.8 copy.16
Async XLA Ops:
  227.5 3.2 %copy-start.2 = (bf16[2,64,2048]{2,1,0:T(8,128)(2,1)S(1)}, bf16[2,64,2048]{2,1,0:T(8,128)(2,1)}, u32[]{:S(2)}) copy-start(bf16[2,64,2048]{2,1,0:T(8,128)(2,1)} %get-tuple-element.17) | copy-start | bytes 1572868
  227.5 3.9 %copy-start.1 = (bf16[2,64,2048]{2,1,0:T(8,128)(2,1)S(1)}, bf16[2,64,2048]{2,1,0:T(8,128)(2,1)}, u32[]{:S(2)}) copy-start(bf16[2,64,2048]{2,1,0:T(8,128)(2,1)} %get-tuple-element.18) | copy-start | bytes 1572868
  230.6 1.6 copy-start

commit v3 on v2

--- a/solution.py
+++ b/solution.py
@@ -1,4 +1,5 @@
 import functools
+import math
 
 import jax
 import jax.numpy as jnp
@@ -25,9 +26,9 @@
 
 
 def kernel(
-    n, x_ref, dy_ref, wg_ref, wu_ref, wd_ref, dx_ref, dwg_ref, dwu_ref, dwd_ref, kept,
+    n, reps, x_ref, dy_ref, wg_ref, wu_ref, wd_ref, dx_ref, dwg_ref, dwu_ref, dwd_ref, kept,
     wgu, wdn, h, g, gt, a, at, act, dgu, da, term, sbuf, rbuf, outg, outu, outd,
-    load_sem, keep_sem, ag_send, ag_recv, sw_send, sw_recv, rs_send, rs_recv,
+    load_sem, keep_sem, ag_send, ag_recv, sw_send, sw_recv, y_send, y_recv, far_send, far_recv, rs_send, rs_recv,
 ):
     layers, _, d_model, ff = wgu.shape
     tokens = h.shape[1]
@@ -46,6 +47,10 @@
     left, right = lax.rem(me + n - 1, n), lax.rem(me + 1, n)
     core = lax.rem(rep, 2)
     partner = rep + 1 - 2 * core
+    sides, across = [], []
+    for stride in (2, 2 * math.isqrt(reps // 2)):
+        sides.append(lax.rem(rep // stride, 2))
+        across.append(rep + stride - 2 * stride * sides[-1])
     toward = ({"dp": left}, {"dp": right})
 
     def at_distance(direction, k):
@@ -65,69 +70,103 @@
         c.start()
 
     barrier = pltpu.get_barrier_semaphore()
-    for other in (*toward, {"rep": partner}):
+    for other in (*toward, {"rep": partner}, *({"rep": r} for r in across)):
         pl.semaphore_signal(barrier, inc=1, device_id=other, device_id_type=MESH)
-    pl.semaphore_wait(barrier, 3)
-
-    def piece(unit, origin, member, part=None):
+    pl.semaphore_wait(barrier, 5)
+
+    def axis(unit):
+        return sum(divmod(unit, SEGMENTS + 1)) % 2
+
+    def share(unit, other_core=False, other_side=False):
+        c, side = 1 - core if other_core else core, sides[axis(unit)]
+        return 2 * (1 - side if other_side else side) + c
+
+    def piece(unit, direction, k, member):
+        origin = at_distance(1 - direction, k)
         l, s = unit // (SEGMENTS + 1), unit % (SEGMENTS + 1)
+        parts = 4
+        halved = k == half
         if s < SEGMENTS:
-            size, first, width = rows // 2, s * seg, seg
-            if part is not None:
+            size, first, width = rows // parts, s * seg, seg
+            if halved:
                 width = seg // 2
-                first += part * width
+                first += direction * width
             row = pl.multiple_of(origin * rows + member * size, size)
             return wgu.at[l, :, pl.ds(row, size), pl.ds(first, width)]
-        size = drows // 2
+        size = drows // parts
         row = origin * drows + member * size
-        if part is not None:
+        if halved:
             size //= 2
-            row += part * size
+            row += direction * size
         return wdn.at[l, pl.ds(pl.multiple_of(row, size), size), :]
+
+    def ship(sems, unit, direction, k, ref, to):
+        send, recv = sems
+        return pltpu.make_async_remote_copy(
+            ref, ref, send.at[unit, direction, k], recv.at[unit, direction, k], device_id=to, device_id_type=MESH
+        )
 
     def hop(unit, direction, k):
         origin = at_distance(1 - direction, k)
-        ref = piece(unit, origin, core, direction if k == half - 1 else None)
-        return pltpu.make_async_remote_copy(
-            ref, ref, ag_send.at[unit, direction, k], ag_recv.at[unit, direction, k],
-            device_id=toward[direction], device_id_type=MESH,
-        )
+        ref = piece(unit, direction, k, share(unit))
+        if k == half - 1:
+            ref = last_half(unit, direction, origin)
+        return ship((ag_send, ag_recv), unit, direction, k, ref, toward[direction])
+
+    def last_half(unit, direction, origin):
+        l, s = unit // (SEGMENTS + 1), unit % (SEGMENTS + 1)
+        parts, member = 4, share(unit)
+        if s < SEGMENTS:
+            size, width = rows // parts, seg // 2
+            row = pl.multiple_of(origin * rows + member * size, size)
+            return wgu.at[l, :, pl.ds(row, size), pl.ds(s * seg + direction * width, width)]
+        size = drows // parts // 2
+        row = origin * drows + (2 * member + direction) * size
+        return wdn.at[l, pl.ds(pl.multiple_of(row, size), size), :]
 
     def landed(unit, direction, k):
-        origin = at_distance(1 - direction, k + 1)
-        ref = piece(unit, origin, core, direction if k == half - 1 else None)
-        return pltpu.make_async_remote_copy(
-            ref, ref, ag_send.at[unit, direction, k], ag_recv.at[unit, direction, k],
-            device_id=toward[direction], device_id_type=MESH,
-        )
-
-    def swap(unit, direction, k, member):
-        origin = at_distance(1 - direction, k + 1)
-        ref = piece(unit, origin, member, direction if k == half - 1 else None)
-        return pltpu.make_async_remote_copy(
-            ref, ref, sw_send.at[unit, direction, k], sw_recv.at[unit, direction, k],
-            device_id={"rep": partner}, device_id_type=MESH,
-        )
+        ref = piece(unit, direction, k + 1, share(unit))
+        return ship((ag_send, ag_recv), unit, direction, k, ref, toward[direction])
+
+    def swap(unit, direction, k, other_core=False):
+        ref = piece(unit, direction, k + 1, share(unit, other_core))
+        return ship((sw_send, sw_recv), unit, direction, k, ref, {"rep": partner})
+
+    def cross(unit, direction, k, other_side=False):
+        ref = piece(unit, direction, k + 1, share(unit, False, other_side))
+        return ship((y_send, y_recv), unit, direction, k, ref, {"rep": across[axis(unit)]})
+
+    def far(unit, direction, k, other_core=False):
+        ref = piece(unit, direction, k + 1, share(unit, other_core, True))
+        return ship((far_send, far_recv), unit, direction, k, ref, {"rep": partner})
 
     def gather(unit, k):
         for direction in range(2):
-            if k > 0:
+            if 0 < k <= half:
                 landed(unit, direction, k - 1).wait_recv()
             if k < half:
                 hop(unit, direction, k).start()
-            if k > 0:
-                swap(unit, direction, k - 1, core).start()
+            if 0 < k <= half:
+                cross(unit, direction, k - 1).start()
+                swap(unit, direction, k - 1).start()
+        if k > 1:
+            for direction in range(2):
+                cross(unit, direction, k - 2, True).wait_recv()
+                far(unit, direction, k - 2).start()
 
     def gathered(unit):
         for k in range(half):
             for direction in range(2):
-                swap(unit, direction, k, 1 - core).wait_recv()
+                swap(unit, direction, k, True).wait_recv()
+                far(unit, direction, k, True).wait_recv()
 
     def close(unit):
         for k in range(half):
             for direction in range(2):
                 hop(unit, direction, k).wait_send()
-                swap(unit, direction, k, core).wait_send()
+                swap(unit, direction, k).wait_send()
+                cross(unit, direction, k).wait_send()
+                far(unit, direction, k).wait_send()
 
     def place(u):
         step = jnp.minimum(u // per_layer, layers - 1)
@@ -228,7 +267,7 @@
     def both(l, columns):
         return jnp.concatenate([wgu[l, 0, :, columns], wgu[l, 1, :, columns]], 1)
 
-    def forward(l, s):
+    def forward(l, s, *between):
         @pl.loop(0, seg // chunk)
         def _(j):
             columns = pl.ds(pl.multiple_of(s * seg + j * chunk, chunk), chunk)
@@ -238,6 +277,9 @@
                 out = dot(a[ts, :], w)
                 gate, up = out[:, :chunk], out[:, chunk:]
                 act[ts, columns] = (gate * jax.nn.sigmoid(gate) * up).astype(BF16)
+            for number, steps in enumerate(between):
+                if steps:
+                    pl.when(j == number)(functools.partial(gathers, *steps))
 
     def down_forward(l):
         part = 2 * tile if tokens % (2 * tile) == 0 else tile
@@ -302,44 +344,56 @@
             g[ts, :] = (g[ts, :].astype(F32) + by_wide.astype(BF16).astype(F32)).astype(BF16)
 
     per = SEGMENTS + 1
+
+    def gathers(*pairs):
+        for unit, k in pairs:
+            gather(unit, k)
+
     for c in loads[1:4]:
         c.wait()
-    for unit in range(per):
-        gather(unit, 0)
+    gathers((0, 0), (1, 0))
     loads[0].wait()
     normed(0)
-    for k in range(1, half):
-        for unit in range(per):
-            gather(unit, k)
+    gathers((0, 1), (1, 1))
+    gathers((0, 2), (1, 2), (2, 0))
+    gathers((0, 3), (1, 3), (2, 1))
     for c in loads[4:]:
         c.wait()
     keeps = []
     for l in range(layers):
+        first, second, down = (l * per + i for i in range(per))
+        last = l + 1 == layers
+        ahead = () if last else ((first + per, 0), (second + per, 0))
+        gathers(*ahead, (first, 4), (second, 4), (down, 2))
+        if l > 0:
+            normed(l)
+        gather(first, 5)
         for c in keeps:
             c.wait()
         keeps = []
-        for s in range(SEGMENTS):
-            unit = l * per + s
-            gather(unit, half)
-            if l + 1 < layers:
-                for later in range(unit + per - s, unit + 2 * per - s):
-                    gather(later, s)
-            gathered(unit)
-            forward(l, s)
-            if l + 1 < layers:
+
+        def keep(s):
+            if not last:
                 columns = pl.ds(s * seg, seg)
                 keeps.append(pltpu.make_async_copy(act.at[:, columns], kept.at[l, :, columns], keep_sem.at[s]))
                 keeps[-1].start()
-        unit = l * per + SEGMENTS
-        gather(unit, half)
-        gathered(unit)
-        if l + 1 < layers:
-            for k in range(SEGMENTS, half):
-                for later in range(unit + 1, unit + 1 + per):
-                    gather(later, k)
-                if k == SEGMENTS:
-                    down_forward(l)
-            normed(l + 1)
+
+        def ahead(*steps):
+            return () if last else tuple((i + per, k) for i, k in steps)
+
+        gathered(first)
+        forward(
+            l, 0, ((second, 5), (down, 3)), ahead((first, 1), (second, 1)), ((down, 4),), ahead((down, 0))
+        )
+        keep(0)
+        gathered(second)
+        forward(
+            l, 1, ahead((first, 2), (second, 2)), ((down, 5),), ahead((down, 1)), ahead((first, 3), (second, 3))
+        )
+        keep(1)
+        gathered(down)
+        if not last:
+            down_forward(l)
 
     for step, l in enumerate(reversed(range(layers))):
         start = step * per_layer
@@ -400,7 +454,7 @@
         any_space = pl.BlockSpec(memory_space=pl.ANY)
         dma = pltpu.SemaphoreType.DMA
         return pl.pallas_call(
-            functools.partial(kernel, n),
+            functools.partial(kernel, n, mesh.shape["rep"]),
             out_shape=[
                 *(jax.ShapeDtypeStruct(t.shape, t.dtype) for t in (x, wg, wu, wd)),
                 jax.ShapeDtypeStruct((layers - 1, tokens, ff), BF16),
@@ -430,6 +484,10 @@
                 dma((gather_units, 2, half)),
                 dma((gather_units, 2, half)),
                 dma((gather_units, 2, half)),
+                dma((gather_units, 2, half)),
+                dma((gather_units, 2, half)),
+                dma((gather_units, 2, half)),
+                dma((gather_units, 2, half)),
                 dma((2, half, SEND)),
                 dma((2, half, RECV)),
             ],

time: 233 us -> 219 us (0.940)
  Pallas kernels: 227 us -> 213 us
    pallas_call x1, Pallas kernels: 227 us -> 213 us  [step(): pl.pallas_call(functools.partial(kernel, n, mesh.shape['rep']), out_shape...]
where the time goes in v3:
time: 219 us
  Pallas kernels  213 us (97%)
  local copies, waits for them, and re-layouts  5.52 us (3%)
    pallas_call x1, Pallas kernels, step(): pl.pallas_call(functools.partial(kernel, n, mesh.shape['rep']), out_shape...  213 us
    unnamed x10, local copies, waits for them, and re-layouts  5.52 us

profile of v3, /device:TPU:28, one launch (start us, length us, event | category | flops | bytes accessed | tf_op | source)
XLA Modules:
  0.0 218.9 jit_solution(8448277539246093100)
XLA Ops:
  0.6 212.8 %shard_map.84 = (bf16[1,2048,512]{2,1,0:T(8,128)(2,1)}, bf16[2,64,2048]{2,1,0:T(8,128)(2,1)}, bf16[2,64,2048]{2,1,0:T(8,128)(2,1)}, bf16[2,256,512]{2,1,0:T(8,128)(2,1)}, bf16[1,2048,2048]{2,1,0:T(8,128)(2,1)}) custom-call(bf16[1,2048,512]{2,1,0:T(8,128)(2,1)} %x_ref.1, bf16[1,2048,512]{2,1,0:T(8,128)(2,1)} %dy_ref.1, bf16[2,64,2048]{2,1,0:T(8,128)(2,1)} %wg_ref.1, ...), custom_call_target="tpu_custom_call" | custom-call | tf_op jit(solution)/shard_map/pallas_call | solution.py:456
  213.4 0.0 copy-start.2
  213.4 0.0 copy-start.1
  213.4 3.1 %copy.13 = bf16[1,2048,512]{2,1,0:T(8,128)(2,1)} copy(bf16[1,2048,512]{2,1,0:T(8,128)(2,1)} %get-tuple-element.16) | data formatting | bytes 4194304
  216.5 0.0 copy-done.2
  216.5 0.0 copy-start
  216.6 0.8 copy.14
  217.3 0.0 copy-done.1
  217.3 0.8 copy.15
  218.1 0.0 copy-done
  218.1 0.8 copy.16
Async XLA Ops:
  213.4 3.2 %copy-start.2 = (bf16[2,64,2048]{2,1,0:T(8,128)(2,1)S(1)}, bf16[2,64,2048]{2,1,0:T(8,128)(2,1)}, u32[]{:S(2)}) copy-start(bf16[2,64,2048]{2,1,0:T(8,128)(2,1)} %get-tuple-element.17) | copy-start | bytes 1572868
  213.4 3.9 %copy-start.1 = (bf16[2,64,2048]{2,1,0:T(8,128)(2,1)S(1)}, bf16[2,64,2048]{2,1,0:T(8,128)(2,1)}, u32[]{:S(2)}) copy-start(bf16[2,64,2048]{2,1,0:T(8,128)(2,1)} %get-tuple-element.18) | copy-start | bytes 1572868
  216.5 1.6 copy-start

commit v4 on v3

--- a/solution.py
+++ b/solution.py
@@ -11,10 +11,10 @@
 MESH = pl.DeviceIdType.MESH
 F32, BF16 = jnp.float32, jnp.bfloat16
 SEGMENTS = 2
-SLOTS = 5
+SLOTS = 7
 RECV = 8
-SEND = 3
-LAG = 2
+SEND = 4
+LAG = 3
 
 
 def dot(a, b):
@@ -38,8 +38,9 @@
     chunks = ff // chunk
     subs = drows // rows
     half = n // 2
-    early = 2
-    per_layer = 1 + 2 * chunks + subs - early
+    lead = subs - 1
+    changing = 3
+    per_layer = lead + 2 * chunks + changing
     dbase = SLOTS * d_model
     seg = ff // SEGMENTS
 
@@ -170,15 +171,17 @@
 
     def place(u):
         step = jnp.minimum(u // per_layer, layers - 1)
-        v = u - step * per_layer
         l = layers - 1 - step
         last = step == layers - 1
-        soon = jnp.where(last, subs, early)
-        odd = lax.rem(v, 2) == 1
-        held = v - 2 * chunks - 1
-        down = (v == 0) | (odd & (v < 2 * soon - 1)) | ((held >= 0) & jnp.logical_not(last))
-        gate = jnp.logical_not(odd) & (v > 0) & (held < 0)
-        index = jnp.where(down, jnp.where(held >= 0, held + early, (v + 1) // 2), v // 2 - 1)
+        first = jnp.where(last, 1, lead)
+        v = u - step * per_layer
+        r = v - first
+        held = r - 2 * chunks
+        even = lax.rem(jnp.maximum(r, 0), 2) == 0
+        beside = last & even & (r >= 0) & (r < 2 * (subs - 1))
+        down = (r < 0) | beside | ((held == 0) & jnp.logical_not(last))
+        gate = jnp.logical_not(even) & (r > 0) & (held < 0)
+        index = jnp.where(r < 0, v, jnp.where(held == 0, lead, jnp.where(beside, 1 + r // 2, r // 2)))
         slot = lax.rem(step * chunks + jnp.maximum(index, 0), SLOTS)
         base = jnp.where(down, dbase + l * ff + index * rows, slot * d_model)
         stride = jnp.where(down, drows, rows)
@@ -291,7 +294,7 @@
                 out = dot(act[ts, :], wdn[l]).astype(BF16)
                 h[l + 1, ts, :] = (h[l, ts, :].astype(F32) + out.astype(F32)).astype(BF16)
 
-    def down_gradient(l):
+    def down_gradient(l, start):
         @pl.loop(0, chunks // 2)
         def _(i):
             for p in range(2):
@@ -299,6 +302,8 @@
                 columns = pl.ds(pl.multiple_of(j * chunk, chunk), chunk)
                 out = dot(gt[...], act[:, columns])
                 term[pl.ds(pl.multiple_of(dbase + l * ff + j * chunk, chunk), chunk), :] = out.T
+            if start > 0:
+                pl.when(i == 1)(functools.partial(tick, start - 1))
 
     def backward_tokens(l, j):
         columns = pl.ds(pl.multiple_of(j * chunk, chunk), chunk)
@@ -354,79 +359,72 @@
     gathers((0, 0), (1, 0))
     loads[0].wait()
     normed(0)
-    gathers((0, 1), (1, 1))
-    gathers((0, 2), (1, 2), (2, 0))
-    gathers((0, 3), (1, 3), (2, 1))
-    for c in loads[4:]:
+    for c in loads[4:-1]:
         c.wait()
+    gathers((2, 0), (3, 0), (0, 1), (1, 1), (2, 1), (3, 1), (0, 2), (1, 2), (2, 2), (3, 2), (0, 3), (4, 0), (1, 3))
+    loads[-1].wait()
+    turn()
+    gathers((2, 3), (5, 0), (3, 3), (0, 4), (4, 1), (1, 4), (2, 4), (5, 1), (0, 5), (3, 4))
+    between = (
+        (((1, 5), (4, 2)), (), ((2, 5), (5, 2)), ((3, 5),)),
+        ((), ((4, 3),), (), ((5, 3),)),
+        (((4, 4),), ((5, 4),), (), ((4, 5), (5, 5))),
+        (),
+    )
     keeps = []
     for l in range(layers):
-        first, second, down = (l * per + i for i in range(per))
         last = l + 1 == layers
-        ahead = () if last else ((first + per, 0), (second + per, 0))
-        gathers(*ahead, (first, 4), (second, 4), (down, 2))
         if l > 0:
             normed(l)
-        gather(first, 5)
         for c in keeps:
             c.wait()
         keeps = []
-
-        def keep(s):
+        for i in range(SEGMENTS):
+            gathered(l * per + i)
+            forward(l, i, *between[l * SEGMENTS + i])
             if not last:
-                columns = pl.ds(s * seg, seg)
-                keeps.append(pltpu.make_async_copy(act.at[:, columns], kept.at[l, :, columns], keep_sem.at[s]))
+                columns = pl.ds(i * seg, seg)
+                keeps.append(pltpu.make_async_copy(act.at[:, columns], kept.at[l, :, columns], keep_sem.at[i]))
                 keeps[-1].start()
-
-        def ahead(*steps):
-            return () if last else tuple((i + per, k) for i, k in steps)
-
-        gathered(first)
-        forward(
-            l, 0, ((second, 5), (down, 3)), ahead((first, 1), (second, 1)), ((down, 4),), ahead((down, 0))
-        )
-        keep(0)
-        gathered(second)
-        forward(
-            l, 1, ahead((first, 2), (second, 2)), ((down, 5),), ahead((down, 1)), ahead((first, 3), (second, 3))
-        )
-        keep(1)
-        gathered(down)
+        gathered(l * per + SEGMENTS)
         if not last:
             down_forward(l)
 
     for step, l in enumerate(reversed(range(layers))):
         start = step * per_layer
-        turn()
+        count = lead if l > 0 else 1
+        da[...] = jnp.zeros_like(da)
         if step > 0:
+            turn()
             normed(l)
-            tick(start - 1)
+            tick(start - 2)
             back.wait()
-        da[...] = jnp.zeros_like(da)
-        down_gradient(l)
+        down_gradient(l, start)
         if l > 0:
             back = pltpu.make_async_copy(kept.at[l - 1], act, keep_sem.at[SEGMENTS])
             back.start()
-        tick(start)
+
+        @pl.loop(0, count)
+        def _(i):
+            tick(start + i)
 
         @pl.loop(0, chunks)
         def _(j):
             backward_tokens(l, j)
-            tick(start + 1 + 2 * j)
+            tick(start + count + 2 * j)
             gate_up_gradient(step, j)
-            tick(start + 2 + 2 * j)
+            tick(start + count + 1 + 2 * j)
 
         norm_backward(l)
         if l > 0:
-            for i in range(subs - early - 1):
-                tick(start + 1 + 2 * chunks + i)
+            tick(start + count + 2 * chunks)
 
     out_dx = pltpu.make_async_copy(g, dx_ref.at[0], load_sem.at[0])
     out_dx.start()
 
     @pl.loop(0, LAG * half)
     def _(i):
-        tick((layers - 1) * per_layer + 2 * chunks + 1 + i)
+        tick((layers - 1) * per_layer + 1 + 2 * chunks + i)
 
     outs = [
         pltpu.make_async_copy(outg, dwg_ref, load_sem.at[1]),

time: 219 us -> 209 us (0.954)
  Pallas kernels: 213 us -> 203 us
    pallas_call x1, Pallas kernels: 213 us -> 203 us  [step(): pl.pallas_call(functools.partial(kernel, n, mesh.shape['rep']), out_shape...]
where the time goes in v4:
time: 209 us
  Pallas kernels  203 us (97%)
  local copies, waits for them, and re-layouts  5.52 us (3%)
    pallas_call x1, Pallas kernels, step(): pl.pallas_call(functools.partial(kernel, n, mesh.shape['rep']), out_shape...  203 us
    unnamed x10, local copies, waits for them, and re-layouts  5.52 us

profile of v4, /device:TPU:28, one launch (start us, length us, event | category | flops | bytes accessed | tf_op | source)
XLA Modules:
  0.0 208.7 jit_solution(11074878411841691675)
XLA Ops:
  0.6 202.5 %shard_map.84 = (bf16[1,2048,512]{2,1,0:T(8,128)(2,1)}, bf16[2,64,2048]{2,1,0:T(8,128)(2,1)}, bf16[2,64,2048]{2,1,0:T(8,128)(2,1)}, bf16[2,256,512]{2,1,0:T(8,128)(2,1)}, bf16[1,2048,2048]{2,1,0:T(8,128)(2,1)}) custom-call(bf16[1,2048,512]{2,1,0:T(8,128)(2,1)} %x_ref.1, bf16[1,2048,512]{2,1,0:T(8,128)(2,1)} %dy_ref.1, bf16[2,64,2048]{2,1,0:T(8,128)(2,1)} %wg_ref.1, ...), custom_call_target="tpu_custom_call" | custom-call | tf_op jit(solution)/shard_map/pallas_call | solution.py:454
  203.2 0.0 copy-start.2
  203.2 0.0 copy-start.1
  203.2 3.1 %copy.13 = bf16[1,2048,512]{2,1,0:T(8,128)(2,1)} copy(bf16[1,2048,512]{2,1,0:T(8,128)(2,1)} %get-tuple-element.16) | data formatting | bytes 4194304
  206.3 0.0 copy-done.2
  206.3 0.0 copy-start
  206.3 0.8 copy.14
  207.1 0.0 copy-done.1
  207.1 0.8 copy.15
  207.9 0.0 copy-done
  207.9 0.8 copy.16
Async XLA Ops:
  203.2 3.2 %copy-start.2 = (bf16[2,64,2048]{2,1,0:T(8,128)(2,1)S(1)}, bf16[2,64,2048]{2,1,0:T(8,128)(2,1)}, u32[]{:S(2)}) copy-start(bf16[2,64,2048]{2,1,0:T(8,128)(2,1)} %get-tuple-element.17) | copy-start | bytes 1572868
  203.2 3.9 %copy-start.1 = (bf16[2,64,2048]{2,1,0:T(8,128)(2,1)S(1)}, bf16[2,64,2048]{2,1,0:T(8,128)(2,1)}, u32[]{:S(2)}) copy-start(bf16[2,64,2048]{2,1,0:T(8,128)(2,1)} %get-tuple-element.18) | copy-start | bytes 1572868
  206.3 1.6 copy-start

commit v5 on v4

--- a/solution.py
+++ b/solution.py
@@ -364,6 +364,7 @@
     gathers((2, 0), (3, 0), (0, 1), (1, 1), (2, 1), (3, 1), (0, 2), (1, 2), (2, 2), (3, 2), (0, 3), (4, 0), (1, 3))
     loads[-1].wait()
     turn()
+    da[...] = jnp.zeros_like(da)
     gathers((2, 3), (5, 0), (3, 3), (0, 4), (4, 1), (1, 4), (2, 4), (5, 1), (0, 5), (3, 4))
     between = (
         (((1, 5), (4, 2)), (), ((2, 5), (5, 2)), ((3, 5),)),
@@ -393,8 +394,8 @@
     for step, l in enumerate(reversed(range(layers))):
         start = step * per_layer
         count = lead if l > 0 else 1
-        da[...] = jnp.zeros_like(da)
         if step > 0:
+            da[...] = jnp.zeros_like(da)
             turn()
             normed(l)
             tick(start - 2)
@@ -451,7 +452,7 @@
         gather_units = layers * (SEGMENTS + 1)
         any_space = pl.BlockSpec(memory_space=pl.ANY)
         dma = pltpu.SemaphoreType.DMA
-        return pl.pallas_call(
+        grads = pl.pallas_call(
             functools.partial(kernel, n, mesh.shape["rep"]),
             out_shape=[
                 *(jax.ShapeDtypeStruct(t.shape, t.dtype) for t in (x, wg, wu, wd)),
@@ -493,6 +494,22 @@
                 collective_id=0, has_side_effects=True, vmem_limit_bytes=67043328
             ),
         )(x, dy, wg, wu, wd)[:4]
+        steps = 4
+
+        def settle(*refs):
+            for source, to in zip(refs[:4], refs[4:]):
+                to[...] = source[...]
+
+        blocks = [
+            pl.BlockSpec((t.shape[0], t.shape[1] // steps, t.shape[2]), lambda i: (0, i, 0)) for t in grads
+        ]
+        return pl.pallas_call(
+            settle,
+            grid=(steps,),
+            in_specs=blocks,
+            out_specs=blocks,
+            out_shape=[jax.ShapeDtypeStruct(t.shape, t.dtype) for t in grads],
+        )(*grads)
 
     tokens_spec, weight_spec = P(("rep", "dp"), None, None), P(None, "dp", None)
     grad_spec = P("rep", "dp", None)

time: 209 us -> 208 us (level)
  local copies, waits for them, and re-layouts: 5.52 us -> 0 us
  Pallas kernels: 203 us -> 207 us
    unnamed x10 -> x0, local copies, waits for them, and re-layouts: 5.52 us -> none
    pallas_call x0 -> x1, Pallas kernels: none -> 4.36 us  [step(): pl.pallas_call(settle, grid=(steps,), in_specs=blocks, out_specs=blocks,...]
where the time goes in v5:
time: 208 us; the launch traced here: 207 us
  Pallas kernels  207 us (100%)
    pallas_call x1, Pallas kernels, step(): pl.pallas_call(functools.partial(kernel, n, mesh.shape['rep']), out_shape...  202 us
    pallas_call x1, Pallas kernels, step(): pl.pallas_call(settle, grid=(steps,), in_specs=blocks, out_specs=blocks,...  4.36 us

profile of v5, /device:TPU:28, one launch (start us, length us, event | category | flops | bytes accessed | tf_op | source)
XLA Modules:
  0.0 207.4 jit_solution(12037780482423256242)
XLA Ops:
  0.6 202.3 %shard_map.84 = (bf16[1,2048,512]{2,1,0:T(8,128)(2,1)}, bf16[2,64,2048]{2,1,0:T(8,128)(2,1)}, bf16[2,64,2048]{2,1,0:T(8,128)(2,1)}, bf16[2,256,512]{2,1,0:T(8,128)(2,1)}, bf16[1,2048,2048]{2,1,0:T(8,128)(2,1)}) custom-call(bf16[1,2048,512]{2,1,0:T(8,128)(2,1)} %x_ref.1, bf16[1,2048,512]{2,1,0:T(8,128)(2,1)} %dy_ref.1, bf16[2,64,2048]{2,1,0:T(8,128)(2,1)} %wg_ref.1, ...), custom_call_target="tpu_custom_call" | custom-call | tf_op jit(solution)/shard_map/pallas_call | solution.py:455
  202.9 4.4 %shard_map.85 = (bf16[1,2048,512]{2,1,0:T(8,128)(2,1)}, bf16[2,64,2048]{2,1,0:T(8,128)(2,1)}, bf16[2,64,2048]{2,1,0:T(8,128)(2,1)}, bf16[2,256,512]{2,1,0:T(8,128)(2,1)}) custom-call(bf16[1,2048,512]{2,1,0:T(8,128)(2,1)} %get-tuple-element.8.refs_0_, bf16[2,64,2048]{2,1,0:T(8,128)(2,1)} %get-tuple-element.9.refs_1_, ...), custom_call_target="tpu_custom_call" | custom-call | tf_op jit(solution)/shard_map/pallas_call | solution.py:506
